TPU v7x, 32 devices: a whole 2x2x4 slice. The times are simulated.
32 devices in a mesh: grp: 8 (over z, core), blk: 4 (over y, x).
Axes of the slice: x: 2, y: 2, z: 4, core: 2. Of those that a mesh axis runs over, the one named last changes fastest.
Arguments:
- integrals: bfloat16 [8, 128, 128, 128], P(None, 'blk'), may hold values from -0.5 to 0.5
- doubles: bfloat16 [64, 128, 128], P('blk'), may hold values from -0.0059814453 to 0.0059814453
- coulomb: bfloat16 [64, 128, 128], P('blk'), may hold values from -0.1796875 to 0.1796875
- singles: float32 [8, 128], P(None, 'blk'), may hold values from -0.18 to 0.18
- occ_energy: float32 [8], replicated, may hold values from -2 to -0.5
- vir_energy: float32 [128], replicated, may hold values from 0.3 to 3
- triplets: int32 [8, 16, 3], P('grp'), may hold values from 0 to 7
- tile_count: int32 [8], P('grp'), may hold values from 1 to 16, as said below
Outputs:
- triplet_energy: float32 [8, 16], P('grp')
- mean_energy: float32 [], replicated
Inputs may be any that keep to these rules, and one draw needn't show every extreme that they name: `tile_count`: slots with an index below a group's count are live; some group has all 16 slots live.
All inputs are finite; a program needn't handle non-finite values.
Results may differ from a plain program's by a relative error of at most 0.0003.
Values may be sent and summed in bfloat16 or wider, within the bound.
A program may use at most 64 MiB of HBM per device.

v0:
```python
import functools

import jax
import jax.numpy as jnp
from jax import lax
from jax.experimental import pallas as pl
from jax.experimental.pallas import tpu as pltpu
from jax.sharding import PartitionSpec as P

MESH = pl.DeviceIdType.MESH


def team_count(occupied, rows, groups):
    teams = occupied
    while teams > 1 and (occupied % teams or rows % teams or groups % (2 * teams)):
        teams -= 1
    return teams


def gather_kernel(n, groups, teams, occupied, doubles_ref, coulomb_ref, codes_ref, dp_ref, cp_ref, all_ref,
                  local_sem, send_sem, recv_sem, fsend_sem, frecv_sem, csend_sem, crecv_sem):
    g = lax.axis_index("grp")
    q = lax.axis_index("blk")
    rows, width = doubles_ref.shape[0], doubles_ref.shape[1]
    runs = rows // teams
    half = width // 2
    team = g // (groups // teams)
    core = g % 2
    partner = g + 1 - 2 * core
    mine = pl.ds(pl.multiple_of(core * half, half), half)
    arrays = ((doubles_ref, dp_ref), (coulomb_ref, cp_ref))

    barrier = pltpu.get_barrier_semaphore()
    for dg in range(1, groups):
        pl.semaphore_signal(barrier, inc=1, device_id={"grp": (g + dg) % groups}, device_id_type=MESH)
    for dq in range(1, n):
        pl.semaphore_signal(barrier, inc=1, device_id={"blk": (q + dq) % n}, device_id_type=MESH)

    def own_row(m):
        j = (q * rows + teams * m) // occupied
        return teams * m + (team + occupied * teams - j) % teams

    locals_ = []
    for m in range(runs):
        for x, (src, dst) in enumerate(arrays):
            copy = pltpu.make_async_copy(src.at[own_row(m)], dst.at[q * runs + m], local_sem.at[m, x])
            copy.start()
            locals_.append(copy)
    all_ref[pl.ds(g, 1)] = codes_ref[...]
    pl.semaphore_wait(barrier, groups - 1 + n - 1)

    code_copies = []
    for dg in range(1, groups):
        copy = pltpu.make_async_remote_copy(
            src_ref=codes_ref.at[0], dst_ref=all_ref.at[g], send_sem=csend_sem.at[dg - 1], recv_sem=crecv_sem.at[dg - 1],
            device_id={"grp": (g + dg) % groups}, device_id_type=MESH)
        copy.start()
        code_copies.append(copy)
    sends = []
    for m in range(runs):
        for x, (src, dst) in enumerate(arrays):
            for dq in range(1, n):
                copy = pltpu.make_async_remote_copy(
                    src_ref=src.at[own_row(m), mine], dst_ref=dst.at[q * runs + m, mine],
                    send_sem=send_sem.at[m, x, dq - 1], recv_sem=recv_sem.at[m, x, dq - 1],
                    device_id={"blk": (q + dq) % n}, device_id_type=MESH)
                copy.start()
                sends.append(copy)
    forwards = []
    at = 0
    for m in range(runs):
        for x, (src, dst) in enumerate(arrays):
            for dq in range(1, n):
                sends[at].wait_recv()
                at += 1
                piece = dst.at[((q + n - dq) % n) * runs + m, mine]
                copy = pltpu.make_async_remote_copy(
                    src_ref=piece, dst_ref=piece,
                    send_sem=fsend_sem.at[m, x, dq - 1], recv_sem=frecv_sem.at[m, x, dq - 1],
                    device_id={"grp": partner}, device_id_type=MESH)
                copy.start()
                forwards.append(copy)
    for copy in locals_:
        copy.wait()
    for copy in sends:
        copy.wait_send()
    for copy in forwards:
        copy.wait()
    for copy in code_copies:
        copy.wait()


def compute_kernel(groups, slots, teams, occupied, unroll, codes, singles, occ, vir, integrals_ref, dp_ref, cp_ref,
                   row_ref, out_ref, vbc_ref, slab_ref, list_g, list_s, sems):
    g = lax.axis_index("grp")
    q = lax.axis_index("blk")
    size = groups // teams
    team, member = g // size, g % size
    blocks, width = integrals_ref.shape[1], integrals_ref.shape[2]

    def scan(index, carry):
        count, turn = carry
        other = index // slots
        slot = index % slots
        ours = codes[other, 0, 3 * slots + slot] == team
        list_g[count] = other
        list_s[count] = slot
        take = jnp.logical_and(ours, turn == member)
        after = jnp.where(turn + 1 == size, 0, turn + 1)
        return count + take.astype(jnp.int32), jnp.where(ours, after, turn)

    count, _ = lax.fori_loop(0, groups * slots, scan, (jnp.int32(0), jnp.int32(0)), unroll=4)

    def fetch(at, buf):
        i = codes[list_g[at], 0, list_s[at]]
        return pltpu.make_async_copy(integrals_ref.at[i], slab_ref.at[buf], sems.at[buf])

    @pl.when(count > 0)
    def _():
        fetch(0, 0).start()

    across = jnp.broadcast_to(row_ref[...], (width, width))
    vbc_ref[...] = across + across.T
    out_ref[...] = jnp.zeros_like(out_ref)
    rows = lax.broadcasted_iota(jnp.int32, out_ref.shape, 0)
    lanes = lax.broadcasted_iota(jnp.int32, out_ref.shape, 1)
    contract = (((1,), (1,)), ((), ()))

    def step(at, carry):
        buf = at % 2
        other, slot = list_g[at], list_s[at]
        i = codes[other, 0, slot]
        j = codes[other, 0, slots + slot]
        k = codes[other, 0, 2 * slots + slot]
        jk = (j * occupied + k) // teams
        kj = (k * occupied + j) // teams
        occ_sum = occ[i] + occ[j] + occ[k]

        @pl.when(at + 1 < count)
        def _():
            fetch(at + 1, 1 - buf).start()

        fetch(at, buf).wait()
        d_jk = dp_ref[jk]
        d_kj = dp_ref[kj]

        def one(a, total):
            block = slab_ref[buf, a]
            left = jnp.concatenate([block, d_jk], axis=1)
            right = jnp.concatenate([d_kj, block], axis=1)
            connected = lax.dot_general(left, right, contract, preferred_element_type=jnp.float32)
            full = connected + singles[i, a] * cp_ref[jk].astype(jnp.float32)
            denominator = (occ_sum - vir[q * blocks + a]) - vbc_ref[...]
            value = full * full / denominator
            return total + jnp.sum(value.reshape(width // 8, 8, width), axis=0)

        total = lax.fori_loop(0, blocks, one, jnp.zeros((8, width), jnp.float32), unroll=unroll)
        here = jnp.logical_and(rows == other, lanes == slot)
        out_ref[...] += jnp.where(here, jnp.sum(total), 0.0)
        return carry

    lax.fori_loop(0, count, step, 0)


def reduce_kernel(n, groups, slots, part_ref, trip_ref, mean_ref, blk_buf, grp_buf, send_sem, recv_sem, gsend_sem, grecv_sem,
                  stage_ref):
    g = lax.axis_index("grp")
    q = lax.axis_index("blk")
    barrier = pltpu.get_barrier_semaphore()
    for dg in range(1, groups):
        pl.semaphore_signal(barrier, inc=1, device_id={"grp": (g + dg) % groups}, device_id_type=MESH)
    for dq in range(1, n):
        pl.semaphore_signal(barrier, inc=1, device_id={"blk": (q + dq) % n}, device_id_type=MESH)
    pl.semaphore_wait(barrier, groups - 1 + n - 1)
    copies = []
    for dq in range(1, n):
        copy = pltpu.make_async_remote_copy(
            src_ref=part_ref, dst_ref=blk_buf.at[q], send_sem=send_sem.at[dq - 1], recv_sem=recv_sem.at[dq - 1],
            device_id={"blk": (q + dq) % n}, device_id_type=MESH)
        copy.start()
        copies.append(copy)
    blk_buf[q] = part_ref[...]
    for copy in copies:
        copy.wait()
    stage = jnp.sum(blk_buf[...], axis=0)
    stage_ref[...] = stage
    grp_buf[g] = stage
    copies = []
    for dg in range(1, groups):
        copy = pltpu.make_async_remote_copy(
            src_ref=stage_ref, dst_ref=grp_buf.at[g], send_sem=gsend_sem.at[dg - 1], recv_sem=grecv_sem.at[dg - 1],
            device_id={"grp": (g + dg) % groups}, device_id_type=MESH)
        copy.start()
        copies.append(copy)
    for copy in copies:
        copy.wait()
    table = jnp.sum(grp_buf[...], axis=0)
    rows = lax.broadcasted_iota(jnp.int32, table.shape, 0)
    trip_ref[...] = jnp.sum(jnp.where(rows == g, table, 0.0), axis=0, keepdims=True)
    mean_ref[...] = jnp.sum(table, keepdims=True) / (groups * slots)


def body(n, groups, integrals, doubles, coulomb, singles, occ_energy, vir_energy, triplets, tile_count):
    occupied, _, width, _ = integrals.shape
    rows = doubles.shape[0]
    slots = triplets.shape[1]
    teams = team_count(occupied, rows, groups)
    runs = rows // teams
    pairs = n * runs
    f32, i32 = jnp.float32, jnp.int32
    vmem = pl.BlockSpec(memory_space=pltpu.VMEM)
    smem = pl.BlockSpec(memory_space=pltpu.SMEM)
    hbm = pl.BlockSpec(memory_space=pl.ANY)
    dma = pltpu.SemaphoreType.DMA

    indices = triplets[0].T
    live = jnp.arange(slots, dtype=i32) < tile_count[0]
    team = jnp.where(live, (indices[1] + indices[2]) % teams, -1)
    codes = jnp.concatenate([indices, team[None]], axis=0).reshape(1, 1, 4 * slots)
    lanes = -(-4 * slots // 128) * 128
    codes = jnp.pad(codes, ((0, 0), (0, 0), (0, lanes - 4 * slots)))

    packed = jax.ShapeDtypeStruct((pairs, width, width), doubles.dtype)
    dp, cp, codes_all = pl.pallas_call(
        functools.partial(gather_kernel, n, groups, teams, occupied),
        out_shape=(packed, packed, jax.ShapeDtypeStruct((groups, 1, lanes), i32)),
        in_specs=[hbm, hbm, vmem],
        out_specs=(vmem, vmem, vmem),
        scratch_shapes=[
            dma((runs, 2)), dma((runs, 2, n - 1)), dma((runs, 2, n - 1)), dma((runs, 2, n - 1)), dma((runs, 2, n - 1)),
            dma((groups - 1,)), dma((groups - 1,)),
        ],
        compiler_params=pltpu.CompilerParams(collective_id=0, has_side_effects=True),
        name="gather",
    )(doubles, coulomb, codes)

    blocks = integrals.shape[1]
    part = pl.pallas_call(
        functools.partial(compute_kernel, groups, slots, teams, occupied, blocks),
        out_shape=jax.ShapeDtypeStruct((groups, slots), f32),
        in_specs=[smem, smem, smem, smem, hbm, vmem, vmem, vmem],
        out_specs=vmem,
        scratch_shapes=[
            pltpu.VMEM((width, width), f32), pltpu.VMEM((2, blocks, width, width), integrals.dtype),
            pltpu.SMEM((groups * slots + 1,), i32), pltpu.SMEM((groups * slots + 1,), i32), dma((2,)),
        ],
        name="energy",
    )(codes_all, singles, occ_energy, vir_energy, integrals, dp, cp, vir_energy.reshape(1, width))

    trip, mean = pl.pallas_call(
        functools.partial(reduce_kernel, n, groups, slots),
        out_shape=(jax.ShapeDtypeStruct((1, slots), f32), jax.ShapeDtypeStruct((1, 1), f32)),
        in_specs=[vmem],
        out_specs=(vmem, vmem),
        scratch_shapes=[
            pltpu.VMEM((n, groups, slots), f32), pltpu.VMEM((groups, groups, slots), f32),
            dma((n - 1,)), dma((n - 1,)), dma((groups - 1,)), dma((groups - 1,)), pltpu.VMEM((groups, slots), f32),
        ],
        compiler_params=pltpu.CompilerParams(collective_id=1, has_side_effects=True),
        name="join",
    )(part)
    return trip, mean.reshape(())


def solution(mesh):
    in_specs = (
        P(None, "blk", None, None),
        P("blk", None, None),
        P("blk", None, None),
        P(None, "blk"),
        P(),
        P(),
        P("grp", None, None),
        P("grp"),
    )
    out_specs = (P("grp", None), P())
    step = functools.partial(body, mesh.shape["blk"], mesh.shape["grp"])
    return jax.shard_map(step, mesh=mesh, in_specs=in_specs, out_specs=out_specs, check_vma=False)
```

profile of v0, /device:TPU:0, one launch (start us, length us, event | category | flops | bytes accessed | tf_op | source)
XLA Modules:
  0.0 51.7 jit_solution(7494912384412686362)
XLA Ops:
  1.3 0.7 %copy.12 = s32[1,16,3]{1,2,0:T(4,128)S(1)} copy(s32[1,16,3]{1,0,2:T(1,128)} %param.14) | data formatting | bytes 384
  2.0 0.1 reshape.20
  2.1 0.5 %pad.4.codes_ref = s32[1,1,128]{2,1,0:T(1,128)} pad(s32[1,1,64]{2,1,0:T(1,128)S(1)} %reshape.20, s32[]{:T(128)} %constant.14.clone.1), padding=0_0x0_0x0_64 | pad | bytes 772 | tf_op jit(solution)/shard_map/jit(_pad)/pad | solution.py:221
  2.6 17.7 %gather.1 = (bf16[16,128,128]{2,1,0:T(8,128)(2,1)}, bf16[16,128,128]{2,1,0:T(8,128)(2,1)}, s32[8,1,128]{2,1,0:T(1,128)}) custom-call(bf16[16,128,128]{2,1,0:T(8,128)(2,1)} %doubles_ref.1, bf16[16,128,128]{2,1,0:T(8,128)(2,1)} %coulomb_ref.1, s32[1,1,128]{2,1,0:T(1,128)} %pad.4.codes_ref), custom_call_target="tpu_custom_call" | custom-call | tf_op jit(solution)/shard_map/gather/pallas_call | solution.py:224
  20.3 16.1 %energy.1.part_ref = f32[8,16]{1,0:T(8,128)} custom-call(s32[8,1,128]{2,1,0:T(1,128)} %get-tuple-element.7.codes, f32[8,32]{1,0:T(8,128)} %singles.1, f32[8]{0:T(128)} %occ.1, f32[128]{0:T(128)} %vir.1, bf16[8,32,128,128]{3,2,1,0:T(8,128)(2,1)} %integrals_ref.1, bf16[16,128,128]{2,1,0:T(8,128)(2,1)} %get-tuple-element.8.dp_ref, ...), custom_call_target="tpu_custom_call" | custom-call | tf_op jit(solution)/shard_map/energy/pallas_call | solution.py:238
  36.4 12.4 %join.1 = (f32[1,16]{1,0:T(1,128)}, f32[1,1]{1,0:T(1,128)}) custom-call(f32[8,16]{1,0:T(8,128)} %energy.1.part_ref), custom_call_target="tpu_custom_call" | custom-call | tf_op jit(solution)/shard_map/join/pallas_call | solution.py:250
  48.8 1.1 %copy.16 = f32[1,16]{1,0:T(1,128)} copy(f32[1,16]{1,0:T(1,128)} %get-tuple-element.14) | data formatting | bytes 128
  (2 shorter events, 0.0 us)
where the time goes:
time: 50.8 us; the launch traced here: 51.7 us
  Pallas kernels  46.2 us (91%)
  between operations  3.07 us (6%)
  local copies, waits for them, and re-layouts  2.42 us (5%)
    pallas_call x1, Pallas kernels, body(): pl.pallas_call(functools.partial(gather_kernel, n, groups, teams, occupie...  17.7 us
    pallas_call x1, Pallas kernels, body(): pl.pallas_call(functools.partial(compute_kernel, groups, slots, teams, oc...  16.1 us
    pallas_call x1, Pallas kernels, body(): pl.pallas_call(functools.partial(reduce_kernel, n, groups, slots), out_sh...  12.4 us
    unnamed x2, local copies, waits for them, and re-layouts  1.82 us

commit v1 on v0

--- a/solution.py
+++ b/solution.py
@@ -17,8 +17,8 @@
     return teams
 
 
-def gather_kernel(n, groups, teams, occupied, doubles_ref, coulomb_ref, codes_ref, dp_ref, cp_ref, all_ref,
-                  local_sem, send_sem, recv_sem, fsend_sem, frecv_sem, csend_sem, crecv_sem):
+def gather_kernel(n, groups, teams, occupied, slots, doubles_ref, coulomb_ref, integrals_ref, trip_ref, live_ref, dp_ref, cp_ref,
+                  held_ref, list_ref, count_ref, all_ref, held_sem, local_sem, send_sem, recv_sem, fsend_sem, frecv_sem, csend_sem, crecv_sem):
     g = lax.axis_index("grp")
     q = lax.axis_index("blk")
     rows, width = doubles_ref.shape[0], doubles_ref.shape[1]
@@ -46,26 +46,59 @@
             copy = pltpu.make_async_copy(src.at[own_row(m)], dst.at[q * runs + m], local_sem.at[m, x])
             copy.start()
             locals_.append(copy)
-    all_ref[pl.ds(g, 1)] = codes_ref[...]
+    held = pltpu.make_async_copy(integrals_ref, held_ref, held_sem)
+    held.start()
+    i, j, k = trip_ref[0], trip_ref[1], trip_ref[2]
+    cube = occupied * occupied * occupied
+    owner = lax.rem(j + k, jnp.full_like(j, teams))
+    code = owner * cube + (i * occupied + j) * occupied + k
+    live = lax.broadcasted_iota(jnp.int32, code.shape, 1) < live_ref[0]
+    all_ref[g] = jnp.full((1, all_ref.shape[2]), -1, jnp.int32)
+    all_ref[g, :, :slots] = jnp.where(live, code, -1)
     pl.semaphore_wait(barrier, groups - 1 + n - 1)
 
     code_copies = []
     for dg in range(1, groups):
         copy = pltpu.make_async_remote_copy(
-            src_ref=codes_ref.at[0], dst_ref=all_ref.at[g], send_sem=csend_sem.at[dg - 1], recv_sem=crecv_sem.at[dg - 1],
+            src_ref=all_ref.at[g], dst_ref=all_ref.at[g], send_sem=csend_sem.at[dg - 1], recv_sem=crecv_sem.at[dg - 1],
             device_id={"grp": (g + dg) % groups}, device_id_type=MESH)
         copy.start()
         code_copies.append(copy)
     sends = []
     for m in range(runs):
         for x, (src, dst) in enumerate(arrays):
+            locals_[m * 2 + x].wait()
             for dq in range(1, n):
                 copy = pltpu.make_async_remote_copy(
-                    src_ref=src.at[own_row(m), mine], dst_ref=dst.at[q * runs + m, mine],
+                    src_ref=dst.at[q * runs + m, mine], dst_ref=dst.at[q * runs + m, mine],
                     send_sem=send_sem.at[m, x, dq - 1], recv_sem=recv_sem.at[m, x, dq - 1],
                     device_id={"blk": (q + dq) % n}, device_id_type=MESH)
                 copy.start()
                 sends.append(copy)
+    for copy in code_copies:
+        copy.wait()
+    table = all_ref[:, 0, :]
+    ours = jnp.logical_and(table >= team * cube, table < (team + 1) * cube).astype(jnp.int32)
+    inner = table - team * cube
+    group_ids = lax.broadcasted_iota(jnp.int32, (groups, 1), 0)
+    totals = jnp.sum(ours, axis=1, keepdims=True)
+    before = jnp.zeros((groups, 1), jnp.int32)
+    for other in range(groups):
+        before += jnp.where(group_ids > other, totals[other:other + 1], 0)
+    size = groups // teams
+    member = g % size
+    places = lax.broadcasted_iota(jnp.int32, (groups, list_ref.shape[1]), 1) * size + member
+    listed = jnp.zeros(places.shape, jnp.int32)
+    for slot in range(slots):
+        column = ours[:, slot:slot + 1]
+        value = (group_ids * slots + slot) * cube + inner[:, slot:slot + 1]
+        rank = jnp.where(column > 0, before, -1)
+        listed += jnp.where(places == rank, value, 0)
+        before += column
+    list_ref[...] = jnp.sum(listed, axis=0, keepdims=True)
+    whole = jnp.sum(totals, axis=0, keepdims=True)
+    count_ref[...] = jnp.broadcast_to((whole - member + size - 1) // size, count_ref.shape)
+
     forwards = []
     at = 0
     for m in range(runs):
@@ -80,44 +113,25 @@
                     device_id={"grp": partner}, device_id_type=MESH)
                 copy.start()
                 forwards.append(copy)
-    for copy in locals_:
-        copy.wait()
+    held.wait()
     for copy in sends:
         copy.wait_send()
     for copy in forwards:
         copy.wait()
-    for copy in code_copies:
-        copy.wait()
-
-
-def compute_kernel(groups, slots, teams, occupied, unroll, codes, singles, occ, vir, integrals_ref, dp_ref, cp_ref,
-                   row_ref, out_ref, vbc_ref, slab_ref, list_g, list_s, sems):
-    g = lax.axis_index("grp")
+
+
+def compute_kernel(groups, slots, teams, occupied, unroll, listed, counts, singles, occ, vir, integrals_ref, dp_ref, cp_ref,
+                   row_ref, out_ref, vbc_ref):
     q = lax.axis_index("blk")
-    size = groups // teams
-    team, member = g // size, g % size
     blocks, width = integrals_ref.shape[1], integrals_ref.shape[2]
-
-    def scan(index, carry):
-        count, turn = carry
-        other = index // slots
-        slot = index % slots
-        ours = codes[other, 0, 3 * slots + slot] == team
-        list_g[count] = other
-        list_s[count] = slot
-        take = jnp.logical_and(ours, turn == member)
-        after = jnp.where(turn + 1 == size, 0, turn + 1)
-        return count + take.astype(jnp.int32), jnp.where(ours, after, turn)
-
-    count, _ = lax.fori_loop(0, groups * slots, scan, (jnp.int32(0), jnp.int32(0)), unroll=4)
-
-    def fetch(at, buf):
-        i = codes[list_g[at], 0, list_s[at]]
-        return pltpu.make_async_copy(integrals_ref.at[i], slab_ref.at[buf], sems.at[buf])
-
-    @pl.when(count > 0)
-    def _():
-        fetch(0, 0).start()
+    count = counts[0, 0]
+
+    def decode(at):
+        code = listed[0, at]
+        k = lax.rem(code, occupied)
+        j = lax.rem(lax.div(code, occupied), occupied)
+        i = lax.rem(lax.div(code, occupied * occupied), occupied)
+        return lax.div(code, occupied * occupied * occupied), i, j, k
 
     across = jnp.broadcast_to(row_ref[...], (width, width))
     vbc_ref[...] = across + across.T
@@ -127,25 +141,17 @@
     contract = (((1,), (1,)), ((), ()))
 
     def step(at, carry):
-        buf = at % 2
-        other, slot = list_g[at], list_s[at]
-        i = codes[other, 0, slot]
-        j = codes[other, 0, slots + slot]
-        k = codes[other, 0, 2 * slots + slot]
-        jk = (j * occupied + k) // teams
-        kj = (k * occupied + j) // teams
+        place, i, j, k = decode(at)
+        other, slot = lax.div(place, slots), lax.rem(place, slots)
         occ_sum = occ[i] + occ[j] + occ[k]
 
-        @pl.when(at + 1 < count)
-        def _():
-            fetch(at + 1, 1 - buf).start()
-
-        fetch(at, buf).wait()
+        jk = lax.div(j * occupied + k, teams)
+        kj = lax.div(k * occupied + j, teams)
         d_jk = dp_ref[jk]
         d_kj = dp_ref[kj]
 
         def one(a, total):
-            block = slab_ref[buf, a]
+            block = integrals_ref[i, a]
             left = jnp.concatenate([block, d_jk], axis=1)
             right = jnp.concatenate([d_kj, block], axis=1)
             connected = lax.dot_general(left, right, contract, preferred_element_type=jnp.float32)
@@ -210,42 +216,39 @@
     f32, i32 = jnp.float32, jnp.int32
     vmem = pl.BlockSpec(memory_space=pltpu.VMEM)
     smem = pl.BlockSpec(memory_space=pltpu.SMEM)
-    hbm = pl.BlockSpec(memory_space=pl.ANY)
+    hbm = pl.BlockSpec(memory_space=pltpu.HBM)
     dma = pltpu.SemaphoreType.DMA
 
-    indices = triplets[0].T
-    live = jnp.arange(slots, dtype=i32) < tile_count[0]
-    team = jnp.where(live, (indices[1] + indices[2]) % teams, -1)
-    codes = jnp.concatenate([indices, team[None]], axis=0).reshape(1, 1, 4 * slots)
-    lanes = -(-4 * slots // 128) * 128
-    codes = jnp.pad(codes, ((0, 0), (0, 0), (0, lanes - 4 * slots)))
+    row_bytes = pairs * width * width * doubles.dtype.itemsize
+    spare = 1 << 20
+    keep = integrals.size * integrals.dtype.itemsize + 2 * row_bytes + 2 * spare
+    lanes = -(-slots // 128) * 128
+    length = -(-groups * slots // 128) * 128
 
     packed = jax.ShapeDtypeStruct((pairs, width, width), doubles.dtype)
-    dp, cp, codes_all = pl.pallas_call(
-        functools.partial(gather_kernel, n, groups, teams, occupied),
-        out_shape=(packed, packed, jax.ShapeDtypeStruct((groups, 1, lanes), i32)),
-        in_specs=[hbm, hbm, vmem],
-        out_specs=(vmem, vmem, vmem),
+    dp, cp, held, listed, counts = pl.pallas_call(
+        functools.partial(gather_kernel, n, groups, teams, occupied, slots),
+        out_shape=(packed, packed, jax.ShapeDtypeStruct(integrals.shape, integrals.dtype), jax.ShapeDtypeStruct((1, length), i32), jax.ShapeDtypeStruct((1, 128), i32)),
+        in_specs=[hbm, hbm, hbm, vmem, smem],
+        out_specs=(vmem, vmem, vmem, vmem, vmem),
         scratch_shapes=[
-            dma((runs, 2)), dma((runs, 2, n - 1)), dma((runs, 2, n - 1)), dma((runs, 2, n - 1)), dma((runs, 2, n - 1)),
+            pltpu.VMEM((groups, 1, lanes), i32), dma, dma((runs, 2)), dma((runs, 2, n - 1)), dma((runs, 2, n - 1)), dma((runs, 2, n - 1)), dma((runs, 2, n - 1)),
             dma((groups - 1,)), dma((groups - 1,)),
         ],
-        compiler_params=pltpu.CompilerParams(collective_id=0, has_side_effects=True),
+        compiler_params=pltpu.CompilerParams(collective_id=0, has_side_effects=True, vmem_limit_bytes=keep),
         name="gather",
-    )(doubles, coulomb, codes)
+    )(*(pltpu.with_memory_space_constraint(x, pltpu.HBM) for x in (doubles, coulomb, integrals)), jnp.transpose(triplets, (2, 0, 1)), tile_count)
 
     blocks = integrals.shape[1]
     part = pl.pallas_call(
         functools.partial(compute_kernel, groups, slots, teams, occupied, blocks),
         out_shape=jax.ShapeDtypeStruct((groups, slots), f32),
-        in_specs=[smem, smem, smem, smem, hbm, vmem, vmem, vmem],
+        in_specs=[smem, smem, smem, smem, smem, vmem, vmem, vmem, vmem],
         out_specs=vmem,
-        scratch_shapes=[
-            pltpu.VMEM((width, width), f32), pltpu.VMEM((2, blocks, width, width), integrals.dtype),
-            pltpu.SMEM((groups * slots + 1,), i32), pltpu.SMEM((groups * slots + 1,), i32), dma((2,)),
-        ],
+        scratch_shapes=[pltpu.VMEM((width, width), f32)],
+        compiler_params=pltpu.CompilerParams(vmem_limit_bytes=keep),
         name="energy",
-    )(codes_all, singles, occ_energy, vir_energy, integrals, dp, cp, vir_energy.reshape(1, width))
+    )(listed, counts, singles, occ_energy, vir_energy, held, dp, cp, vir_energy.reshape(1, width))
 
     trip, mean = pl.pallas_call(
         functools.partial(reduce_kernel, n, groups, slots),
@@ -256,7 +259,7 @@
             pltpu.VMEM((n, groups, slots), f32), pltpu.VMEM((groups, groups, slots), f32),
             dma((n - 1,)), dma((n - 1,)), dma((groups - 1,)), dma((groups - 1,)), pltpu.VMEM((groups, slots), f32),
         ],
-        compiler_params=pltpu.CompilerParams(collective_id=1, has_side_effects=True),
+        compiler_params=pltpu.CompilerParams(collective_id=1, has_side_effects=True, vmem_limit_bytes=4 * spare),
         name="join",
     )(part)
     return trip, mean.reshape(())

time: 50.8 us -> 41.7 us (0.82); the launches traced: 51.7 us -> 41.7 us
  Pallas kernels: 46.2 us -> 37.4 us
  local copies, waits for them, and re-layouts: 2.42 us -> 1.2 us
    pallas_call x1, Pallas kernels: 12.4 us -> 8.65 us  [body(): pl.pallas_call(functools.partial(reduce_kernel, n, groups, slots), out_sh...]
    pallas_call x1, Pallas kernels: 16.1 us -> 12.9 us  [body(): pl.pallas_call(functools.partial(compute_kernel, groups, slots, teams, oc...]
    pallas_call x1, Pallas kernels: 17.7 us -> 15.9 us  [body(): pl.pallas_call(functools.partial(gather_kernel, n, groups, teams, occupie...]
    unnamed x2 -> x9, local copies, waits for them, and re-layouts: 1.82 us -> 1.2 us
    pad x1 -> x0, local copies, waits for them, and re-layouts: 0.52 us -> none  [body(): codes = jnp.pad(codes, ((0, 0), (0, 0), (0, lanes - 4 * slots)))]
where the time goes in v1:
time: 41.7 us
  Pallas kernels  37.4 us (90%)
  between operations  3.07 us (7%)
  local copies, waits for them, and re-layouts  1.2 us (3%)
    pallas_call x1, Pallas kernels, body(): pl.pallas_call(functools.partial(gather_kernel, n, groups, teams, occupie...  15.9 us
    pallas_call x1, Pallas kernels, body(): pl.pallas_call(functools.partial(compute_kernel, groups, slots, teams, oc...  12.9 us
    pallas_call x1, Pallas kernels, body(): pl.pallas_call(functools.partial(reduce_kernel, n, groups, slots), out_sh...  8.65 us
    unnamed x9, local copies, waits for them, and re-layouts  1.2 us

profile of v1, /device:TPU:0, one launch (start us, length us, event | category | flops | bytes accessed | tf_op | source)
XLA Modules:
  0.0 41.7 jit_solution(324681296434657809)
XLA Ops:
  0.6 0.0 copy-start.1
  0.6 0.0 copy-start.3
  0.7 0.0 copy-start
  1.3 0.0 copy-start.2
  1.3 0.7 %copy-done.2 = s32[1,16,3]{1,0,2:T(1,128)S(1)} copy-done((s32[1,16,3]{1,0,2:T(1,128)S(1)}, s32[1,16,3]{1,0,2:T(1,128)}, u32[]{:S(2)}) %copy-start.2) | copy-done | bytes 216
  2.0 15.9 %gather.1 = (bf16[16,128,128]{2,1,0:T(8,128)(2,1)S(1)}, bf16[16,128,128]{2,1,0:T(8,128)(2,1)S(1)}, bf16[8,32,128,128]{3,2,1,0:T(8,128)(2,1)S(1)}, s32[1,128]{1,0:T(1,128)S(1)}, s32[1,128]{1,0:T(1,128)S(1)}) custom-call(bf16[16,128,128]{2,1,0:T(8,128)(2,1)} %doubles_ref.1, bf16[16,128,128]{2,1,0:T(8,128)(2,1)} %coulomb_ref.1, ...), custom_call_target="tpu_custom_call" | custom-call | tf_op jit(solution)/shard_map/gather/pallas_call | solution.py:229
  17.9 0.0 copy-done.1
  17.9 0.0 copy-done.3
  17.9 0.0 copy-done
  17.9 12.9 %energy.1.part_ref = f32[8,16]{1,0:T(8,128)S(1)} custom-call(s32[1,128]{1,0:T(1,128)S(1)} %get-tuple-element.9.listed, s32[1,128]{1,0:T(1,128)S(1)} %get-tuple-element.10.counts, f32[8,32]{1,0:T(8,128)S(1)} %copy-done, f32[8]{0:T(128)S(1)} %copy-done.3, f32[128]{0:T(128)S(1)} %copy-done.1, bf16[8,32,128,128]{3,2,1,0:T(8,128)(2,1)S(1)} %get-tuple-element.11.integrals_ref, ...), custom_call_target="tpu_custom_call" | custom-call | tf_op jit(solution)/shard_map/energy/pallas_call | solution.py:243
  30.8 8.7 %join.1 = (f32[1,16]{1,0:T(1,128)S(1)}, f32[1,1]{1,0:T(1,128)}) custom-call(f32[8,16]{1,0:T(8,128)S(1)} %energy.1.part_ref), custom_call_target="tpu_custom_call" | custom-call | tf_op jit(solution)/shard_map/join/pallas_call | solution.py:253
  39.5 0.5 %copy.13 = f32[1,16]{1,0:T(1,128)} copy(f32[1,16]{1,0:T(1,128)S(1)} %get-tuple-element.18) | data formatting | bytes 128
Async XLA Ops:
  0.6 17.3 %copy-start.1 = (f32[128]{0:T(128)S(1)}, f32[128]{0:T(128)}, u32[]{:S(2)}) copy-start(f32[128]{0:T(128)} %vir.1) | copy-start | bytes 1540
  0.6 17.3 %copy-start.3 = (f32[8]{0:T(128)S(1)}, f32[8]{0:T(128)}, u32[]{:S(2)}) copy-start(f32[8]{0:T(128)} %occ.1) | copy-start | bytes 100
  0.7 17.3 %copy-start = (f32[8,32]{1,0:T(8,128)S(1)}, f32[8,32]{1,0:T(8,128)}, u32[]{:S(2)}) copy-start(f32[8,32]{1,0:T(8,128)} %singles.1) | copy-start | bytes 3076
  1.3 0.7 %copy-start.2 = (s32[1,16,3]{1,0,2:T(1,128)S(1)}, s32[1,16,3]{1,0,2:T(1,128)}, u32[]{:S(2)}) copy-start(s32[1,16,3]{1,0,2:T(1,128)} %param.14) | copy-start | bytes 580
